TPU v7x, 256 devices: a whole 4x4x8 slice. The times are simulated.
256 devices in a mesh: node: 8 (over x, core), chip: 32 (over y, z).
Axes of the slice: x: 4, y: 4, z: 8, core: 2. Of those that a mesh axis runs over, the one named last changes fastest.
Arguments:
- table: float32 [2, 1048576, 128], P(None, ('node', 'chip')), may hold values from -1.5 to 1.5
- unique_ids: int32 [256, 2, 4096], P(('node', 'chip')), may hold values from 0 to 4095, as said below
- counts: int32 [256, 2, 256], P(('node', 'chip')), may hold values from 12 to 16, as said below
- inverse: int32 [131072, 2, 40], P(('node', 'chip')), may hold values from 0 to 4095, as said below
- lengths: int32 [131072, 2], P(('node', 'chip')), may hold values from 1 to 40
Outputs:
- pooled: float32 [131072, 2, 128], P(('node', 'chip'))
Inputs may be any that keep to these rules, and one draw needn't show every extreme that they name: `counts`: for every device and table some owner receives exactly 16, and for every table some owner receives 16 from every device. `unique_ids`: entries u with offsets[o] <= u < offsets[o] + counts[o] are distinct row numbers of owner o; entries past the total are unused. `inverse`: every entry is below the sum of counts of its device and table.
All inputs are finite; a program needn't handle non-finite values.
Results may differ from a plain program's by a relative error of at most 0.0003.
Values sent between devices are 32-bit elements; how exact they have to be, the bound alone decides.
A program may use at most 64 MiB of HBM per device.

v0:
```python
import jax
import jax.numpy as jnp
from jax import lax
from jax.sharding import PartitionSpec as P


def cut_along(value, dim, count):
    dims = value.shape
    parts = value.reshape(*dims[:dim], count, dims[dim] // count, *dims[dim + 1 :])
    return jnp.moveaxis(parts, dim, 0)


def laid_out(parts, dim):
    dims = list(parts.shape[1:])
    dims[dim] *= parts.shape[0]
    return jnp.moveaxis(parts, 0, dim).reshape(dims)


def exchange_both(value, axis, axes, splits, concats):
    sizes = [lax.axis_size(a) for a in axes]
    parts = cut_along(value, splits[0], sizes[0])
    parts = jnp.moveaxis(cut_along(parts, splits[1] + 1, sizes[1]), 0, 1)
    inside = parts.shape[2:]
    parts = parts.reshape(-1, *inside)
    parts = lax.all_to_all(parts, axis, split_axis=0, concat_axis=0, tiled=True)
    parts = laid_out(parts.reshape(*sizes, *inside), concats[0] + 1)
    return laid_out(parts, concats[1])


def pool_table(slots, inclusive, count, index, lens, capacity):
    owners = inclusive.shape[0]
    samples, depth = index.shape
    owner_ids = jnp.arange(owners, dtype=jnp.int32)
    skipped = jnp.where(owner_ids < owners - 1, capacity - count, 0)
    below = inclusive[None, None, :] <= index[:, :, None]
    slot = index + jnp.sum(jnp.where(below, skipped[None, None, :], 0), axis=2)
    positions = jnp.arange(depth, dtype=jnp.int32)
    live = positions[None, :] < lens[:, None]
    vectors = slots[jnp.where(live, slot, 0)]
    return jnp.sum(jnp.where(live[:, :, None], vectors, jnp.zeros((), jnp.float32)), axis=1)


def local(table, unique_ids, counts, inverse, lengths):
    n_node = lax.axis_size("node")
    n_chip = lax.axis_size("chip")
    owners = n_node * n_chip
    tables, rows_dev, width = table.shape
    capacity = unique_ids.shape[2] // owners
    count = counts[0]
    inclusive = jnp.cumsum(count, axis=1)
    offset = inclusive - count
    within = jnp.arange(capacity, dtype=jnp.int32)
    upos = offset[:, :, None] + within[None, None, :]
    valid = within[None, None, :] < count[:, :, None]
    upos = jnp.where(valid, upos, 0)
    wanted = jnp.take_along_axis(unique_ids[0], upos.reshape(tables, owners * capacity), axis=1)
    wanted = jnp.where(valid.reshape(tables, owners * capacity), wanted, 0)
    wanted = wanted.reshape(tables, n_node, n_chip, capacity)
    outs = []
    for t in range(tables):
        arrived = exchange_both(wanted[t], ("node", "chip"), ("node", "chip"), (0, 1), (0, 1))
        looked = table[t][arrived]
        back = exchange_both(looked, ("node", "chip"), ("node", "chip"), (0, 1), (0, 1))
        slots = back.reshape(owners * capacity, width)
        outs.append(
            pool_table(slots, inclusive[t], count[t], inverse[:, t, :], lengths[:, t], capacity)
        )
    return jnp.stack(outs, axis=1)


def solution(mesh):
    return jax.shard_map(
        local,
        mesh=mesh,
        in_specs=(
            P(None, ("node", "chip"), None),
            P(("node", "chip"), None, None),
            P(("node", "chip"), None, None),
            P(("node", "chip"), None, None),
            P(("node", "chip"), None),
        ),
        out_specs=P(("node", "chip"), None, None),
        check_vma=False,
    )
```

profile of v0, /device:TPU:1, one launch (start us, length us, event | category | flops | bytes accessed | tf_op | source)
XLA Modules:
  0.0 393.0 jit_solution(11891019902246901493)
XLA Ops:
  0.0 0.0 copy-start
  0.0 0.7 reshape.413
  0.7 0.6 reduce-window.6
  1.3 0.2 slice_reduce_fusion.2
  1.5 0.2 reduce-window.9
  1.7 0.1 fusion.5
  1.8 0.7 bitcast_subtract_fusion
  2.5 0.1 add.108
  2.6 0.2 add.113
  2.8 0.2 add.109
  2.9 0.8 lt.190
  3.7 0.2 lt.195
  3.9 0.2 lt.191
  4.1 0.1 lt.187
  4.2 0.1 or_bitcast_fusion
  4.3 69.2 %gather_fusion.4 = s32[8192]{0:T(1024)S(1)} fusion(s32[2,4096]{1,0:T(2,128)S(1)} %bitcast.102, s32[8192]{0:T(1024)S(1)} %bitcast.104), kind=kCustom, calls=%fused_computation.4 | custom fusion | bytes 131072 | tf_op jit(solution)/shard_map/jit(take_along_axis)/gather | solution.py:56
  73.5 0.1 fusion.2
  73.6 0.1 slice_reduce_fusion.1
  73.6 0.8 reshape_transpose_transpose_reshape_reshape_squeeze.7
  74.4 15.6 %all-to-all-start.2 = ((s32[256,1,1,16]{3,2,1,0:T(1,128)}), s32[256,1,1,16]{3,2,1,0:T(1,128)S(1)}, u32[]{:S(2)}, u32[]{:S(2)}) async-start(s32[256,1,1,16]{3,2,1,0:T(1,128)} %bitcast.30), calls=%async_computation.2 | async-start | bytes 262144 | tf_op jit(solution)/shard_map/all_to_all | solution.py:25
  90.1 3.8 slice_bitcast_fusion.1
  93.9 0.7 reshape_transpose_transpose_reshape_reshape_squeeze.6
  94.6 8.4 %all-to-all-done.2 = s32[256,1,1,16]{3,2,1,0:T(1,128)S(1)} async-done(((s32[256,1,1,16]{3,2,1,0:T(1,128)}), s32[256,1,1,16]{3,2,1,0:T(1,128)S(1)}, u32[]{:S(2)}, u32[]{:S(2)}) %all-to-all-start.2) | async-done | bytes 16416 | tf_op jit(solution)/shard_map/all_to_all | solution.py:25
  103.0 5.5 %all-to-all-start = ((s32[256,1,1,16]{3,2,1,0:T(1,128)}), s32[256,1,1,16]{3,2,1,0:T(1,128)S(1)}, u32[]{:S(2)}, u32[]{:S(2)}) async-start(s32[256,1,1,16]{3,2,1,0:T(1,128)} %bitcast.4), calls=%async_computation | async-start | bytes 262144 | tf_op jit(solution)/shard_map/all_to_all | solution.py:25
  108.6 0.1 reshape.443
  108.7 14.1 %gather_fusion.2 = f32[4096,128]{1,0:T(8,128)} fusion(f32[4096,128]{1,0:T(8,128)S(1)} %get-tuple-element.8, s32[4096]{0:T(1024)S(1)} %broadcast_clamp_fusion.2), kind=kCustom, calls=%fused_computation.2 | custom fusion | bytes 4210688 | tf_op jit(solution)/shard_map/gather | solution.py:62
  122.8 0.0 all-to-all-done
  122.8 13.9 %all-to-all-start.3 = ((f32[256,1,1,16,128]{4,3,2,1,0:T(8,128)}), f32[256,1,1,16,128]{4,3,2,1,0:T(8,128)S(1)}, u32[]{:S(2)}, u32[]{:S(2)}) async-start(f32[256,1,1,16,128]{4,3,2,1,0:T(8,128)} %bitcast.108), calls=%async_computation.3 | async-start | bytes 4194304 | tf_op jit(solution)/shard_map/all_to_all | solution.py:25
  136.7 0.1 broadcast_add_fusion
  136.8 0.1 reshape.427
  136.9 15.7 %gather_fusion = f32[4096,128]{1,0:T(8,128)} fusion(f32[4096,128]{1,0:T(8,128)} %get-tuple-element.7, s32[4096]{0:T(1024)S(1)} %broadcast_clamp_fusion.3), kind=kCustom, calls=%fused_computation | custom fusion | bytes 4210688 | tf_op jit(solution)/shard_map/gather | solution.py:62
  152.6 38.5 %all-to-all-done.3 = f32[256,1,1,16,128]{4,3,2,1,0:T(8,128)S(1)} async-done(((f32[256,1,1,16,128]{4,3,2,1,0:T(8,128)}), f32[256,1,1,16,128]{4,3,2,1,0:T(8,128)S(1)}, u32[]{:S(2)}, u32[]{:S(2)}) %all-to-all-start.3) | async-done | bytes 2097184 | tf_op jit(solution)/shard_map/all_to_all | solution.py:25
  191.1 7.0 %all-to-all-start.1 = ((f32[256,1,1,16,128]{4,3,2,1,0:T(8,128)}), f32[256,1,1,16,128]{4,3,2,1,0:T(8,128)}, u32[]{:S(2)}, u32[]{:S(2)}) async-start(f32[256,1,1,16,128]{4,3,2,1,0:T(8,128)} %bitcast.107), calls=%async_computation.1 | async-start | bytes 4194304 | tf_op jit(solution)/shard_map/all_to_all | solution.py:25
  198.2 0.1 copy.26
  198.3 0.1 copy.27
  198.4 24.5 %select_reduce_fusion = (s32[512,40]{1,0:T(8,128)S(1)}, s32[512,40]{1,0:T(8,128)S(1)}) fusion(s32[256]{0:T(256)S(1)} %bitcast.123, s32[512,40]{1,0:T(8,128)S(1)} %bitcast.109, s32[256]{0:T(256)S(1)} %get-tuple-element.14, s32[256]{0:T(256)S(1)} %bitcast.122, s32[512,40]{1,0:T(8,128)S(1)} %bitcast.110, s32[256]{0:T(256)S(1)} %get-tuple-element.13), kind=kLoop, calls=%fused_computation.5 | loop fusion | flops 31416320 | bytes 331776 | tf_op jit(solution)/shard_map/reduce_sum | solution.py:36
  222.9 0.1 compare_select_fusion.1
  223.0 0.2 reshape.435
  223.2 0.1 compare_select_fusion
  223.4 0.2 reshape.451
  223.6 0.1 iota_compare_fusion.1
  223.7 0.1 iota_compare_fusion.3
  223.9 68.0 %gather_fusion.3 = f32[20480,128]{1,0:T(8,128)} fusion(f32[4096,128]{1,0:T(8,128)S(1)} %bitcast.103, s32[20480]{0:T(1024)S(1)} %broadcast_clamp_fusion), kind=kCustom, calls=%fused_computation.3 | custom fusion | bytes 21053440 | tf_op jit(solution)/shard_map/gather | solution.py:39
  291.8 15.2 %select_reduce_fusion.2 = f32[512,128]{1,0:T(8,128)S(1)} fusion(f32[512,40,128]{2,1,0:T(8,128)} %bitcast.105, pred[512,40]{1,0:T(8,128)(4,1)S(1)} %iota_compare_fusion.1), kind=kLoop, calls=%fused_computation.7 | loop fusion | flops 5177344 | bytes 10768384 | tf_op jit(solution)/shard_map/reduce_sum | solution.py:40
  307.0 0.0 all-to-all-done.1
  307.0 69.5 %gather_fusion.1 = f32[20480,128]{1,0:T(8,128)} fusion(f32[4096,128]{1,0:T(8,128)} %bitcast.20, s32[20480]{0:T(1024)S(1)} %broadcast_clamp_fusion.1), kind=kCustom, calls=%fused_computation.1 | custom fusion | bytes 21053440 | tf_op jit(solution)/shard_map/gather | solution.py:39
  376.6 15.2 %select_reduce_fusion.3 = f32[512,128]{1,0:T(8,128)S(1)} fusion(f32[512,40,128]{2,1,0:T(8,128)} %bitcast.106, pred[512,40]{1,0:T(8,128)(4,1)S(1)} %iota_compare_fusion.3), kind=kLoop, calls=%fused_computation.8 | loop fusion | flops 5177344 | bytes 10768384 | tf_op jit(solution)/shard_map/reduce_sum | solution.py:40
  391.7 1.3 pad_maximum_fusion
  (20 shorter events, 0.1 us)
Async XLA Ops:
  0.0 4.3 %copy-start = (s32[1,2,4096]{2,1,0:T(2,128)S(1)}, s32[1,2,4096]{2,1,0:T(2,128)}, u32[]{:S(2)}) copy-start(s32[1,2,4096]{2,1,0:T(2,128)} %param.6) | copy-start | bytes 98308
  74.4 28.6 %all-to-all-start.2 = ((s32[256,1,1,16]{3,2,1,0:T(1,128)}), s32[256,1,1,16]{3,2,1,0:T(1,128)S(1)}, u32[]{:S(2)}, u32[]{:S(2)}) async-start(s32[256,1,1,16]{3,2,1,0:T(1,128)} %bitcast.30), calls=%async_computation.2 | async-start | bytes 262144 | tf_op jit(solution)/shard_map/all_to_all | solution.py:25
  103.0 19.7 %all-to-all-start = ((s32[256,1,1,16]{3,2,1,0:T(1,128)}), s32[256,1,1,16]{3,2,1,0:T(1,128)S(1)}, u32[]{:S(2)}, u32[]{:S(2)}) async-start(s32[256,1,1,16]{3,2,1,0:T(1,128)} %bitcast.4), calls=%async_computation | async-start | bytes 262144 | tf_op jit(solution)/shard_map/all_to_all | solution.py:25
  122.8 13.9 %copy-start.2 = (s32[1,2,256]{2,1,0:T(2,128)S(1)}, s32[1,2,256]{2,1,0:T(2,128)}, u32[]{:S(2)}) copy-start(s32[1,2,256]{2,1,0:T(2,128)} %param.7) | copy-start | bytes 6148
  122.8 14.0 %copy-start.3 = (s32[512,2]{0,1:T(2,128)S(1)}, s32[512,2]{0,1:T(2,128)}, u32[]{:S(2)}) copy-start(s32[512,2]{0,1:T(2,128)} %param.9) | copy-start | bytes 12292
  122.8 14.0 %copy-start.1 = (s32[512,2,40]{0,2,1:T(8,128)S(1)}, s32[512,2,40]{0,2,1:T(8,128)}, u32[]{:S(2)}) copy-start(s32[512,2,40]{0,2,1:T(8,128)} %param.8) | copy-start | bytes 491524
  122.8 68.3 %all-to-all-start.3 = ((f32[256,1,1,16,128]{4,3,2,1,0:T(8,128)}), f32[256,1,1,16,128]{4,3,2,1,0:T(8,128)S(1)}, u32[]{:S(2)}, u32[]{:S(2)}) async-start(f32[256,1,1,16,128]{4,3,2,1,0:T(8,128)} %bitcast.108), calls=%async_computation.3 | async-start | bytes 4194304 | tf_op jit(solution)/shard_map/all_to_all | solution.py:25
  191.1 115.9 %all-to-all-start.1 = ((f32[256,1,1,16,128]{4,3,2,1,0:T(8,128)}), f32[256,1,1,16,128]{4,3,2,1,0:T(8,128)}, u32[]{:S(2)}, u32[]{:S(2)}) async-start(f32[256,1,1,16,128]{4,3,2,1,0:T(8,128)} %bitcast.107), calls=%async_computation.1 | async-start | bytes 4194304 | tf_op jit(solution)/shard_map/all_to_all | solution.py:25
where the time goes:
time: 393 us
  local copies, waits for them, and re-layouts  245 us (62%)
  other arithmetic  58.4 us (15%)
  waiting for transfers between devices  46.9 us (12%)
  starting transfers between devices  42 us (11%)
    gather x2, local copies, waits for them, and re-layouts, pool_table(): vectors = slots[jnp.where(live, slot, 0)]  138 us
    gather x2, local copies, waits for them, and re-layouts, local(): jnp.take_along_axis(unique_ids[0], upos.reshape(tables, owners * capacity...  69.2 us
    all_to_all x4, waiting for transfers between devices, exchange_both(): parts = lax.all_to_all(parts, axis, split_axis=0, concat_axis=0, tiled=True)  46.9 us
    all_to_all x4, starting transfers between devices, exchange_both(): parts = lax.all_to_all(parts, axis, split_axis=0, concat_axis=0, tiled=True)  42 us
    reduce_sum x2, other arithmetic, pool_table(): jnp.sum(jnp.where(live[:, :, None], vectors, jnp.zeros((), jnp.float32)),...  30.3 us
    gather x2, local copies, waits for them, and re-layouts, local(): looked = table[t][arrived]  29.8 us
    reduce_sum x1, other arithmetic, pool_table(): slot = index + jnp.sum(jnp.where(below, skipped[None, None, :], 0), axis=2)  24.5 us
  transfers between devices with their start and end apart: 4, of which 2 were waited for; matrix products, arithmetic and copies ran while one was open for 36% of the time, Pallas kernels for 0%

commit v1 on v0

v1 whole, which is shorter than its diff:
```python
import functools

import jax
import jax.numpy as jnp
from jax import lax
from jax.experimental import pallas as pl
from jax.experimental.pallas import tpu as pltpu
from jax.sharding import PartitionSpec as P

MESH = pl.DeviceIdType.MESH
NZ = 8
CORES = 2
FIELDS = 4
BITS = 8

ROUTES = (
    (4, None, None, None),
    (3, 1, 2, 1),
    (5, -1, 1, 1),
    (2, 0, 2, 0),
    (6, 0, 1, 0),
    (1, 1, 0, 0),
    (7, -1, 0, 2),
    (0, 0, 0, 1),
)


def kernel(
    dims,
    counts,
    ids,
    inv,
    lens,
    table_hbm,
    out,
    table,
    start,
    msg,
    idbuf,
    idnum,
    code,
    code_in,
    group_of,
    unit_of,
    weight,
    send,
    recv,
    acc,
    part,
    ready,
    table_sem,
    id_send,
    id_recv,
    num_sem,
    code_send,
    code_recv,
    row_send,
    row_recv,
    part_send,
    part_recv,
):
    nx, ny, cap, rows_dev = dims
    q_all = nx * CORES * ny
    owners = q_all * NZ
    tables, depth, samples = inv.shape
    slots = q_all * cap
    words = slots // FIELDS
    node, chip = lax.axis_index("node"), lax.axis_index("chip")
    n_node, n_chip = nx * CORES, ny * NZ
    x, c, y, z = node // CORES, node % CORES, chip // NZ, chip % NZ
    mine = node * ny + y

    def place(dx, dy, dc, dz):
        return (
            ((x + dx) % nx) * CORES + (c + dc) % CORES,
            ((y + dy) % ny) * NZ + (z + dz) % NZ,
        )

    def step_of(i):
        return (i // CORES) % nx, i // n_node, i % CORES

    barrier = pltpu.get_barrier_semaphore()
    row = [(node, (chip + i) % n_chip) for i in range(1, n_chip)]
    column = [((node + i) % n_node, chip) for i in range(1, n_node)]
    for peer in row + column:
        pl.semaphore_signal(barrier, inc=1, device_id=peer, device_id_type=MESH)
    fetch = pltpu.make_async_copy(table_hbm, table, table_sem)
    fetch.start()

    def add_up(o, sums):
        new = []
        for t in range(tables):
            start[t, o] = sums[t]
            new.append(sums[t] + counts[t, o])
        return tuple(new)

    lax.fori_loop(0, owners, add_up, (jnp.int32(0),) * tables)

    lane = lax.broadcasted_iota(jnp.int32, (1, 128), 1)
    last = ids.shape[0] - 1

    def write_message(k, _):
        dx, dy, dc = step_of(k % q_all)
        dz = k // q_all
        on, oc = place(-dx, -dy, -dc, -dz)
        o = on * n_chip + oc
        pieces = []
        for t in range(tables):
            at = start[t, o]
            r = jnp.minimum(at >> 7, last)
            l = at & 127
            a = ids[r, pl.ds(t, 1), :]
            b = ids[jnp.minimum(r + 1, last), pl.ds(t, 1), :]
            both = jnp.where(lane < l, b, a)
            pieces.append(pltpu.roll(both, (cap * t - l) & 127, 1))
        line = jnp.where(lane < cap, pieces[0], pieces[1])
        msg[k] = jnp.clip(line, 0, rows_dev - 1)
        return 0

    lax.fori_loop(0, owners, write_message, 0)

    pl.semaphore_wait(barrier, n_chip + n_node - 2)
    for peer in column:
        pl.semaphore_signal(ready, inc=1, device_id=peer, device_id_type=MESH)
    pl.semaphore_wait(ready, n_node - 1)

    def send_ids(k, delta):
        dx, dy, dc = step_of(k % q_all)
        pltpu.make_async_remote_copy(
            msg.at[k],
            idbuf.at[k],
            id_send,
            id_recv.at[delta],
            device_id=place(-dx, -dy, -dc, -delta),
            device_id_type=MESH,
        ).start()

    for delta, _, _, _ in ROUTES:

        def one(i, _, delta=delta):
            send_ids(delta * q_all + i, delta)
            return 0

        lax.fori_loop(1 if delta == 0 else 0, q_all, one, 0)

    position = lax.broadcasted_iota(jnp.int32, (depth, samples), 0)
    for t in range(tables):
        index = inv[t]

        def shift(o, slot, t=t, index=index):
            n = counts[t, o]
            return slot + jnp.where(index >= start[t, o] + n, cap - n, 0)

        slot = lax.fori_loop(0, owners - 1, shift, index, unroll=5)
        plane = (slot // cap) % NZ
        value = plane * slots + (slot // (cap * NZ)) * cap + slot % cap
        code[t] = jnp.where(position < lens[t], value, -1)
    code_copies = []
    for side, dz in ((0, 2), (1, -2)):
        copy = pltpu.make_async_remote_copy(
            code,
            code_in[side],
            code_send.at[side],
            code_recv.at[side],
            device_id=place(0, 0, 0, dz),
            device_id_type=MESH,
        )
        copy.start()
        code_copies.append(copy)

    def split_codes(source, g):
        for t in range(tables):
            v = source[t]
            live = v >= 0
            inside = v % slots
            group_of[g, t] = jnp.where(live, (v // slots) * words + inside % words, -1)
            unit_of[g, t] = jnp.where(live, 1 << (BITS * (inside // words)), 0)

    lanes = min(128, samples)
    rows_at = lax.broadcasted_iota(jnp.int32, (words, lanes), 0)

    def count(w, g, t, plane):
        wanted = rows_at + plane * words

        def tile(i, _):
            at = pl.multiple_of(i * lanes, lanes)

            def step(n, total):
                rows = pl.ds(pl.multiple_of(n * 8, 8), 8)
                groups = group_of.at[g, t, rows, pl.ds(at, lanes)]
                units = unit_of.at[g, t, rows, pl.ds(at, lanes)]
                for p in range(8):
                    hit = groups[pl.ds(p, 1), :] == wanted
                    total = total + jnp.where(hit, units[pl.ds(p, 1), :], 0)
                return total

            total = lax.fori_loop(0, depth // 8, step, jnp.zeros((words, lanes), jnp.int32))
            for f in range(FIELDS):
                part_count = (total >> (BITS * f)) & ((1 << BITS) - 1)
                weight[w, pl.ds(f * words, words), pl.ds(at, lanes)] = part_count.astype(
                    jnp.float32
                ).astype(jnp.bfloat16)
            return 0

        lax.fori_loop(0, samples // lanes, tile, 0)

    works = [[], [], []]
    n_work = 0
    for g, planes in ((0, (-1, 0, 1)), (1, (0, 1, 2)), (2, (0, -1, -2))):
        for b, dz in enumerate(planes):
            for t in range(tables):
                if g and b == 2 and t != g - 1:
                    continue
                works[g].append((b, t, n_work, dz))
                n_work += 1

    split_codes(code, 0)
    for b, t, w, dz in works[0]:
        count(w, 0, t, (z + dz) % NZ)

    def ids_ready(delta):
        rows = pl.ds(delta * q_all, q_all) if delta else pl.ds(1, q_all - 1)
        got = idbuf.at[rows]
        pltpu.make_async_copy(got, got, id_recv.at[delta]).wait()
        copy = pltpu.make_async_copy(got, idnum.at[rows], num_sem.at[delta])
        copy.start()
        return copy

    def collect(k):
        for t in range(tables):
            for s in range(cap):
                r = idnum[k, 0, t * cap + s]
                send[k, t, pl.ds(s, 1), :] = table[t * rows_dev + r]

    def send_rows(k, i, delta, dz, g, b):
        dx, dy, dc = step_of(i)

        def go(source, target, sem, dz):
            pltpu.make_async_remote_copy(
                source,
                target,
                row_send,
                row_recv.at[sem],
                device_id=place(dx, dy, dc, dz),
                device_id_type=MESH,
            ).start()

        if g is None:
            go(send.at[k, 0], recv[5].at[mine], 5, -2)
            go(send.at[k, 1], recv[8].at[mine], 8, 2)
        else:
            go(send.at[k], recv[3 * g + b].at[mine], 3 * g + b, dz)

    own_ids = pltpu.make_async_copy(
        msg.at[pl.ds(0, 1)], idnum.at[pl.ds(0, 1)], num_sem.at[NZ]
    )
    own_ids.start()
    copies = [ids_ready(ROUTES[0][0])]
    copies += [ids_ready(route[0]) for route in ROUTES[1:]]
    fetch.wait()
    own_ids.wait()
    for copy in copies:
        copy.wait()
    for delta, dz, g, b in ROUTES:
        stay = dz == 0
        if stay:
            k0 = delta * q_all
            collect(k0)
            pltpu.make_async_copy(
                send.at[k0], recv[3 * g + b].at[mine], row_recv.at[3 * g + b]
            ).start()

        def serve(i, _, delta=delta, dz=dz, g=g, b=b):
            k = delta * q_all + i
            collect(k)
            send_rows(k, i, delta, dz, g, b)
            return 0

        lax.fori_loop(1 if stay else 0, q_all, serve, 0)

    def rows_ready(g, b):
        got = recv[3 * g + b]
        pltpu.make_async_copy(got, got, row_recv.at[3 * g + b]).wait()

    def pool(g, b, t, w, first):
        block = recv[3 * g + b]
        rows = block[...] if g and b == 2 else block[:, t]
        rows = rows.reshape(slots, 128).T
        high = rows.astype(jnp.bfloat16)
        low = (rows - high.astype(jnp.float32)).astype(jnp.bfloat16)
        both = jnp.dot(
            jnp.concatenate([high, low], axis=0), weight[w], preferred_element_type=jnp.float32
        )
        new = both[:128] + both[128:]
        total = acc[tables * g + t]
        total[...] = new if first else total[...] + new

    part_copies = []
    for g in (1, 2):
        code_copies[g - 1].wait_recv()
        split_codes(code_in[g - 1], g)
        for b, t, w, dz in works[g]:
            count(w, g, t, (z + dz) % NZ)
    for g in (1, 2):
        for b in range(3):
            rows_ready(g, b)
        for t in (2 - g, g - 1):
            todo = [work for work in works[g] if work[1] == t]
            for n, (b, _, w, _) in enumerate(todo):
                pool(g, b, t, w, n == 0)
            copy = pltpu.make_async_remote_copy(
                acc[tables * g + t],
                part[tables * (g - 1) + t],
                part_send.at[g - 1, t],
                part_recv.at[g - 1, t],
                device_id=place(0, 0, 0, -2 if g == 1 else 2),
                device_id_type=MESH,
            )
            copy.start()
            part_copies.append((t, copy))

    done = set()
    for b in (1, 0, 2):
        rows_ready(0, b)
        for bb, t, w, _ in works[0]:
            if bb == b:
                pool(0, b, t, w, t not in done)
                done.add(t)
    for t in range(tables):
        for tt, copy in part_copies:
            if tt == t:
                copy.wait_recv()
        out[t] = (acc[t][...] + (part[t][...] + part[tables + t][...])).T

    for copy in code_copies:
        copy.wait_send()
    for _, copy in part_copies:
        copy.wait_send()
    pltpu.make_async_copy(msg.at[pl.ds(1, owners - 1)], msg.at[pl.ds(1, owners - 1)], id_send).wait()
    sent = send.at[pl.ds(0, owners - 3)]
    pltpu.make_async_copy(sent, sent, row_send).wait()


def local(sizes, table, unique_ids, counts, inverse, lengths):
    nx, ny = sizes
    tables, rows_dev, width = table.shape
    owners = counts.shape[2]
    uniq = unique_ids.shape[2]
    cap = uniq // owners
    samples, _, depth = inverse.shape
    q_all = nx * CORES * ny
    slots = q_all * cap
    dims = (nx, ny, cap, rows_dev)
    vmem = pl.BlockSpec(memory_space=pltpu.VMEM)
    block = pltpu.VMEM((q_all, tables, cap, width), jnp.float32)
    far = pltpu.VMEM((q_all, cap, width), jnp.float32)
    out = pl.pallas_call(
        functools.partial(kernel, dims),
        out_shape=jax.ShapeDtypeStruct((tables, samples, width), jnp.float32),
        in_specs=[
            pl.BlockSpec(memory_space=pltpu.SMEM),
            vmem,
            vmem,
            vmem,
            pl.BlockSpec(memory_space=pl.ANY),
        ],
        out_specs=vmem,
        scratch_shapes=[
            pltpu.VMEM((tables * rows_dev, 1, width), jnp.float32),
            pltpu.SMEM((tables, owners), jnp.int32),
            pltpu.VMEM((owners, 1, 128), jnp.int32),
            pltpu.VMEM((owners, 1, 128), jnp.int32),
            pltpu.SMEM((owners, 1, 128), jnp.int32),
            pltpu.VMEM((tables, depth, samples), jnp.int32),
            [pltpu.VMEM((tables, depth, samples), jnp.int32)] * 2,
            pltpu.VMEM((3, tables, depth, samples), jnp.int32),
            pltpu.VMEM((3, tables, depth, samples), jnp.int32),
            pltpu.VMEM((16, slots, samples), jnp.bfloat16),
            pltpu.VMEM((owners, tables, cap, width), jnp.float32),
            [block, block, block, block, block, far, block, block, far],
            [pltpu.VMEM((width, samples), jnp.float32)] * (3 * tables),
            [pltpu.VMEM((width, samples), jnp.float32)] * (2 * tables),
            pltpu.SemaphoreType.REGULAR,
            pltpu.SemaphoreType.DMA,
            pltpu.SemaphoreType.DMA,
            pltpu.SemaphoreType.DMA((NZ,)),
            pltpu.SemaphoreType.DMA((NZ + 1,)),
            pltpu.SemaphoreType.DMA((2,)),
            pltpu.SemaphoreType.DMA((2,)),
            pltpu.SemaphoreType.DMA,
            pltpu.SemaphoreType.DMA((9,)),
            pltpu.SemaphoreType.DMA((2, 2)),
            pltpu.SemaphoreType.DMA((2, 2)),
        ],
        compiler_params=pltpu.CompilerParams(
            collective_id=0, has_side_effects=True, vmem_limit_bytes=56 << 20
        ),
        name="bags",
    )(
        counts[0],
        unique_ids.reshape(tables, uniq // 128, 128).transpose(1, 0, 2),
        inverse.transpose(1, 2, 0),
        lengths.T.reshape(tables, 1, samples),
        table.reshape(tables * rows_dev, 1, width),
    )
    return out.transpose(1, 0, 2)


def solution(mesh):
    sizes = (mesh.shape["node"] // CORES, mesh.shape["chip"] // NZ)
    return jax.shard_map(
        functools.partial(local, sizes),
        mesh=mesh,
        in_specs=(
            P(None, ("node", "chip"), None),
            P(("node", "chip"), None, None),
            P(("node", "chip"), None, None),
            P(("node", "chip"), None, None),
            P(("node", "chip"), None),
        ),
        out_specs=P(("node", "chip"), None, None),
        check_vma=False,
    )
```

time: 393 us -> 140 us (0.36)
  local copies, waits for them, and re-layouts: 245 us -> 3.52 us
  Pallas kernels: 0 us -> 136 us
  other arithmetic: 58.4 us -> 0 us
  waiting for transfers between devices: 46.9 us -> 0 us
  starting transfers between devices: 42 us -> 0 us
    gather x6 -> x0, local copies, waits for them, and re-layouts: 236 us -> none  [the longest x2 138 us: pool_table(): vectors = slots[jnp.where(live, slot, 0)]]
    pallas_call x0 -> x1, Pallas kernels: none -> 136 us  [local(): pl.pallas_call(functools.partial(kernel, dims), out_shape=jax.ShapeDtypeS...]
    reduce_sum x3 -> x0, other arithmetic: 54.8 us -> none  [the longest x2 30.3 us: pool_table(): jnp.sum(jnp.where(live[:, :, None], vectors, jnp.zeros((), jnp.float32)),...]
    all_to_all x4 -> x0, waiting for transfers between devices: 46.9 us -> none  [exchange_both(): parts = lax.all_to_all(parts, axis, split_axis=0, concat_axis=0, tiled=True)]
    all_to_all x4 -> x0, starting transfers between devices: 42 us -> none  [exchange_both(): parts = lax.all_to_all(parts, axis, split_axis=0, concat_axis=0, tiled=True)]
  transfers between devices with their start and end apart: 4 -> 0, of which waited for: 2 -> 0; matrix products, arithmetic and copies ran while one was open for 36% -> 0% of each run, Pallas kernels for 0% -> 0%
where the time goes in v1:
time: 140 us
  Pallas kernels  136 us (97%)
  local copies, waits for them, and re-layouts  3.52 us (3%)
    pallas_call x1, Pallas kernels, local(): pl.pallas_call(functools.partial(kernel, dims), out_shape=jax.ShapeDtypeS...  136 us

profile of v1, /device:TPU:1, one launch (start us, length us, event | category | flops | bytes accessed | tf_op | source)
XLA Modules:
  0.0 140.0 jit_solution(3315990353293305891)
XLA Ops:
  0.0 1.3 reshape.10.lens
  1.3 136.5 %bags.1 = f32[2,512,128]{2,1,0:T(8,128)} custom-call(s32[2,256]{1,0:T(2,128)} %bitcast.13, s32[32,2,128]{2,1,0:T(2,128)} %bitcast.11, s32[2,40,512]{2,1,0:T(8,128)} %bitcast.10, s32[2,1,512]{2,1,0:T(1,128)} %reshape.10.lens, f32[8192,1,128]{2,1,0:T(1,128)} %bitcast.8), custom_call_target="tpu_custom_call" | custom-call | tf_op jit(solution)/shard_map/bags/pallas_call | solution.py:357
  137.8 2.2 %copy.6 = f32[512,2,128]{2,1,0:T(2,128)} copy(f32[512,2,128]{2,0,1:T(8,128)} %bitcast.9) | data formatting | bytes 1048576 | tf_op jit(solution)/shard_map/transpose | solution.py:406

commit v2 on v1

v2 whole, which is shorter than its diff:
```python
import functools

import jax
import jax.numpy as jnp
from jax import lax
from jax.experimental import pallas as pl
from jax.experimental.pallas import tpu as pltpu
from jax.sharding import PartitionSpec as P

MESH = pl.DeviceIdType.MESH
NZ = 8
CORES = 2
FIELDS = 4
BITS = 8

FAR = (
    ((4, -2, 1, 2), (5, -1, 1, 1), (3, 1, 2, 1), (6, 0, 1, 0), (2, 0, 2, 0)),
    ((4, 2, 2, 2), (3, 1, 2, 1), (5, -1, 1, 1), (2, 0, 2, 0), (6, 0, 1, 0)),
)
NEAR = ((1, 1, 0, 0), (7, -1, 0, 2), (0, 0, 0, 1))
ID_ORDER = (4, 5, 3, 6, 2, 1, 7, 0)


def near_slot(b):
    return b


def far_slot(t, g, b):
    at = [(route[2], route[3]) for route in FAR[t]].index((g, b))
    return len(NEAR) + t * len(FAR[0]) + at


def kernel(
    dims,
    counts,
    ids,
    inv,
    lens,
    table_hbm,
    out,
    table,
    start,
    msg,
    idbuf,
    idnum,
    code,
    code_in,
    group_of,
    unit_of,
    weight,
    send,
    recv,
    acc,
    part,
    ready,
    table_sem,
    id_send,
    id_recv,
    num_sem,
    code_send,
    code_recv,
    row_send,
    row_recv,
    part_send,
    part_recv,
):
    nx, ny, cap, rows_dev = dims
    q_all = nx * CORES * ny
    owners = q_all * NZ
    tables, depth, samples = inv.shape
    slots = q_all * cap
    words = slots // FIELDS
    node, chip = lax.axis_index("node"), lax.axis_index("chip")
    n_node, n_chip = nx * CORES, ny * NZ
    x, c, y, z = node // CORES, node % CORES, chip // NZ, chip % NZ
    mine = node * ny + y

    steps = [(dx, dc) for dx in range(nx) for dc in range(CORES)]
    node_to = [lax.rem(x + dx, nx) * CORES + lax.rem(c + dc, CORES) for dx, dc in steps]
    node_from = [
        lax.rem(x + nx - dx, nx) * CORES + lax.rem(c + CORES - dc, CORES) for dx, dc in steps
    ]

    def chip_at(dy, dz):
        return lax.rem(y + ny + dy, ny) * NZ + lax.rem(z + NZ + dz, NZ)

    def above(dz):
        return node, chip_at(0, dz)

    barrier = pltpu.get_barrier_semaphore()
    row = [(node, (chip + i) % n_chip) for i in range(1, n_chip)]
    column = [((node + i) % n_node, chip) for i in range(1, n_node)]
    for peer in row + column:
        pl.semaphore_signal(barrier, inc=1, device_id=peer, device_id_type=MESH)
    fetch = pltpu.make_async_copy(table_hbm, table, table_sem)
    fetch.start()

    lane = lax.broadcasted_iota(jnp.int32, (1, 128), 1)
    last = ids.shape[0] - 1

    def write_messages(n, sums):
        sums = list(sums)
        for u in range(8):
            o = n * 8 + u
            pieces = []
            for t in range(tables):
                at = sums[t]
                start[t, o] = at
                sums[t] = at + counts[t, o]
                r = jnp.minimum(at >> 7, last)
                l = at & 127
                a = ids[r, pl.ds(t, 1), :]
                b = ids[jnp.minimum(r + 1, last), pl.ds(t, 1), :]
                both = jnp.where(lane < l, b, a)
                pieces.append(pltpu.roll(both, (cap * t - l) & 127, 1))
            line = jnp.where(lane < cap, pieces[0], pieces[1])
            msg[o] = jnp.clip(line, 0, rows_dev - 1)
        return tuple(sums)

    lax.fori_loop(0, owners // 8, write_messages, (jnp.int32(0),) * tables)

    pl.semaphore_wait(barrier, n_chip + n_node - 2)
    for peer in column:
        pl.semaphore_signal(ready, inc=1, device_id=peer, device_id_type=MESH)
    pl.semaphore_wait(ready, n_node - 1)

    def send_ids(delta, dy, j):
        to = (node_from[j], chip_at(-dy, -delta))
        pltpu.make_async_remote_copy(
            msg.at[to[0] * n_chip + to[1]],
            idbuf.at[delta * q_all + dy * n_node + j],
            id_send,
            id_recv.at[delta],
            device_id=to,
            device_id_type=MESH,
        ).start()

    for delta in ID_ORDER:

        def one(dy, _, delta=delta):
            for j in range(n_node):
                if delta == 0 and j == 0:

                    @pl.when(dy > 0)
                    def _():
                        send_ids(delta, dy, j)
                else:
                    send_ids(delta, dy, j)
            return 0

        lax.fori_loop(0, ny, one, 0)

    position = lax.broadcasted_iota(jnp.int32, (depth, samples), 0)
    for t in range(tables):
        index = inv[t]

        def shift(o, slot, t=t, index=index):
            n = counts[t, o]
            return slot + jnp.where(index >= start[t, o] + n, cap - n, 0)

        slot = lax.fori_loop(0, owners - 1, shift, index, unroll=5)
        plane = (slot // cap) % NZ
        value = plane * slots + (slot // (cap * NZ)) * cap + slot % cap
        code[t] = jnp.where(position < lens[pl.ds(t, 1), :], value, -1)
    code_copies = []
    for side, dz in ((0, 2), (1, -2)):
        copy = pltpu.make_async_remote_copy(
            code,
            code_in[side],
            code_send.at[side],
            code_recv.at[side],
            device_id=above(dz),
            device_id_type=MESH,
        )
        copy.start()
        code_copies.append(copy)

    def split_codes(source, g):
        for t in range(tables):
            v = source[t]
            live = v >= 0
            inside = v % slots
            group_of[g, t] = jnp.where(live, (v // slots) * words + inside % words, -1)
            unit_of[g, t] = jnp.where(live, 1 << (BITS * (inside // words)), 0)

    lanes = min(128, samples)
    rows_at = lax.broadcasted_iota(jnp.int32, (words, lanes), 0)

    def count(w, g, t, plane):
        wanted = rows_at + plane * words

        def tile(i, _):
            at = pl.multiple_of(i * lanes, lanes)

            def step(n, total):
                rows = pl.ds(pl.multiple_of(n * 8, 8), 8)
                groups = group_of.at[g, t, rows, pl.ds(at, lanes)]
                units = unit_of.at[g, t, rows, pl.ds(at, lanes)]
                for p in range(8):
                    hit = groups[pl.ds(p, 1), :] == wanted
                    total = total + jnp.where(hit, units[pl.ds(p, 1), :], 0)
                return total

            total = lax.fori_loop(0, depth // 8, step, jnp.zeros((words, lanes), jnp.int32))
            for f in range(FIELDS):
                part_count = (total >> (BITS * f)) & ((1 << BITS) - 1)
                weight[w, pl.ds(f * words, words), pl.ds(at, lanes)] = part_count.astype(
                    jnp.float32
                ).astype(jnp.bfloat16)
            return 0

        lax.fori_loop(0, samples // lanes, tile, 0)

    works = []
    for b in range(3):
        works += [(near_slot(b), 0, t, 2 * b + t, b - 1) for t in range(tables)]
    for t in range(tables):
        for _, _, g, b in FAR[t]:
            works.append((far_slot(t, g, b), g, t, len(works), b if g == 1 else -b))

    def count_all(g, t):
        for _, gg, tt, w, dz in works:
            if (gg, tt) == (g, t):
                count(w, g, t, lax.rem(z + NZ + dz, NZ))

    def ids_ready(delta):
        rows = pl.ds(delta * q_all, q_all) if delta else pl.ds(1, q_all - 1)
        got = idbuf.at[rows]
        pltpu.make_async_copy(got, got, id_recv.at[delta]).wait()
        copy = pltpu.make_async_copy(got, idnum.at[rows], num_sem.at[delta])
        copy.start()
        return copy

    def collect(k, t):
        for s in range(cap):
            r = idnum[k, 0, t * cap + s]
            send[k, t, pl.ds(s, 1), :] = table[t * rows_dev + r]

    def serve(delta, dz, slot, t):
        def piece(k):
            return send.at[k] if t is None else send.at[k, t]

        def send_rows(k, dy, j):
            pltpu.make_async_remote_copy(
                piece(k),
                recv[slot].at[mine],
                row_send,
                row_recv.at[slot],
                device_id=(node_to[j], chip_at(dy, dz)),
                device_id_type=MESH,
            ).start()

        def line(dy, _):
            for j in range(n_node):
                k = delta * q_all + dy * n_node + j
                for tt in range(tables):
                    if t is None or t == tt:
                        collect(k, tt)
                if dz == 0 and j == 0:

                    @pl.when(dy > 0)
                    def _():
                        send_rows(k, dy, j)

                    @pl.when(dy == 0)
                    def _():
                        pltpu.make_async_copy(
                            piece(k), recv[slot].at[mine], row_recv.at[slot]
                        ).start()
                else:
                    send_rows(k, dy, j)
            return 0

        lax.fori_loop(0, ny, line, 0)

    def serve_far(t):
        for delta, dz, g, b in FAR[t]:
            serve(delta, dz, far_slot(t, g, b), t)

    own_ids = pltpu.make_async_copy(
        msg.at[pl.ds(node * n_chip + chip, 1)], idnum.at[pl.ds(0, 1)], num_sem.at[NZ]
    )
    own_ids.start()
    copies = [ids_ready(delta) for delta in ID_ORDER]
    fetch.wait()
    own_ids.wait()
    for copy in copies:
        copy.wait()

    def rows_ready(slot):
        got = recv[slot]
        pltpu.make_async_copy(got, got, row_recv.at[slot]).wait()

    def pool(slot, g, t, w, first):
        rows = recv[slot][:, t] if g == 0 else recv[slot][...]
        rows = rows.reshape(slots, 128).T
        high = rows.astype(jnp.bfloat16)
        low = (rows - high.astype(jnp.float32)).astype(jnp.bfloat16)
        both = jnp.dot(
            jnp.concatenate([high, low], axis=0), weight[w], preferred_element_type=jnp.float32
        )
        new = both[:128] + both[128:]
        total = acc[tables * g + t]
        total[...] = new if first else total[...] + new

    part_copies = []

    def pool_far(t):
        for g in ((1, 2), (2, 1))[t]:
            mine_now = [work for work in works if work[1:3] == (g, t)]
            for n, (slot, _, _, w, _) in enumerate(mine_now):
                rows_ready(slot)
                pool(slot, g, t, w, n == 0)
            copy = pltpu.make_async_remote_copy(
                acc[tables * g + t],
                part[tables * (g - 1) + t],
                part_send.at[g - 1, t],
                part_recv.at[g - 1, t],
                device_id=above(-2 if g == 1 else 2),
                device_id_type=MESH,
            )
            copy.start()
            part_copies.append((t, copy))

    serve_far(0)
    for g in (1, 2):
        code_copies[g - 1].wait_recv()
        split_codes(code_in[g - 1], g)
        count_all(g, 0)
    serve_far(1)
    for g in (1, 2):
        count_all(g, 1)
    pool_far(0)
    for delta, dz, _, b in NEAR:
        serve(delta, dz, near_slot(b), None)
    split_codes(code, 0)
    for t in range(tables):
        count_all(0, t)
    pool_far(1)

    for n, b in enumerate((1, 0, 2)):
        rows_ready(near_slot(b))
        for slot, g, t, w, _ in works:
            if g == 0 and slot == near_slot(b):
                pool(slot, g, t, w, n == 0)
    for t in range(tables):
        for tt, copy in part_copies:
            if tt == t:
                copy.wait_recv()
        out[pl.ds(t, samples, stride=tables), :] = (
            acc[t][...] + (part[t][...] + part[tables + t][...])
        ).T

    for copy in code_copies:
        copy.wait_send()
    for _, copy in part_copies:
        copy.wait_send()
    pltpu.make_async_copy(msg.at[pl.ds(1, owners - 1)], msg.at[pl.ds(1, owners - 1)], id_send).wait()
    sent = send.at[pl.ds(0, owners - 3)]
    pltpu.make_async_copy(sent, sent, row_send).wait()


def local(sizes, table, unique_ids, counts, inverse, lengths):
    nx, ny = sizes
    tables, rows_dev, width = table.shape
    owners = counts.shape[2]
    uniq = unique_ids.shape[2]
    cap = uniq // owners
    samples, _, depth = inverse.shape
    q_all = nx * CORES * ny
    slots = q_all * cap
    dims = (nx, ny, cap, rows_dev)
    vmem = pl.BlockSpec(memory_space=pltpu.VMEM)
    block = pltpu.VMEM((q_all, tables, cap, width), jnp.float32)
    far = pltpu.VMEM((q_all, cap, width), jnp.float32)
    out = pl.pallas_call(
        functools.partial(kernel, dims),
        out_shape=jax.ShapeDtypeStruct((samples * tables, width), jnp.float32),
        in_specs=[
            pl.BlockSpec(memory_space=pltpu.SMEM),
            vmem,
            vmem,
            vmem,
            pl.BlockSpec(memory_space=pl.ANY),
        ],
        out_specs=vmem,
        scratch_shapes=[
            pltpu.VMEM((tables * rows_dev, 1, width), jnp.float32),
            pltpu.SMEM((tables, owners), jnp.int32),
            pltpu.VMEM((owners, 1, 128), jnp.int32),
            pltpu.VMEM((owners, 1, 128), jnp.int32),
            pltpu.SMEM((owners, 1, 128), jnp.int32),
            pltpu.VMEM((tables, depth, samples), jnp.int32),
            [pltpu.VMEM((tables, depth, samples), jnp.int32)] * 2,
            pltpu.VMEM((3, tables, depth, samples), jnp.int32),
            pltpu.VMEM((3, tables, depth, samples), jnp.int32),
            pltpu.VMEM((16, slots, samples), jnp.bfloat16),
            pltpu.VMEM((owners, tables, cap, width), jnp.float32),
            [block] * 3 + [far] * 10,
            [pltpu.VMEM((width, samples), jnp.float32)] * (3 * tables),
            [pltpu.VMEM((width, samples), jnp.float32)] * (2 * tables),
            pltpu.SemaphoreType.REGULAR,
            pltpu.SemaphoreType.DMA,
            pltpu.SemaphoreType.DMA,
            pltpu.SemaphoreType.DMA((NZ,)),
            pltpu.SemaphoreType.DMA((NZ + 1,)),
            pltpu.SemaphoreType.DMA((2,)),
            pltpu.SemaphoreType.DMA((2,)),
            pltpu.SemaphoreType.DMA,
            pltpu.SemaphoreType.DMA((13,)),
            pltpu.SemaphoreType.DMA((2, 2)),
            pltpu.SemaphoreType.DMA((2, 2)),
        ],
        compiler_params=pltpu.CompilerParams(
            collective_id=0, has_side_effects=True, vmem_limit_bytes=56 << 20
        ),
        name="bags",
    )(
        counts[0],
        unique_ids.reshape(tables, uniq // 128, 128).transpose(1, 0, 2),
        inverse.transpose(1, 2, 0),
        lengths.T,
        table.reshape(tables * rows_dev, 1, width),
    )
    return out.reshape(samples, tables, width)


def solution(mesh):
    sizes = (mesh.shape["node"] // CORES, mesh.shape["chip"] // NZ)
    return jax.shard_map(
        functools.partial(local, sizes),
        mesh=mesh,
        in_specs=(
            P(None, ("node", "chip"), None),
            P(("node", "chip"), None, None),
            P(("node", "chip"), None, None),
            P(("node", "chip"), None, None),
            P(("node", "chip"), None),
        ),
        out_specs=P(("node", "chip"), None, None),
        check_vma=False,
    )
```

time: 140 us -> 92.8 us (0.66)
  the two profiles are of different devices: /device:TPU:1 before, /device:TPU:49 now
where the time goes in v2:
time: 92.8 us; the launch traced here: 92.6 us
  Pallas kernels  90.8 us (98%)
  local copies, waits for them, and re-layouts  1.87 us (2%)
    pallas_call x1, Pallas kernels, local(): pl.pallas_call(functools.partial(kernel, dims), out_shape=jax.ShapeDtypeS...  90.8 us
    unnamed x1, local copies, waits for them, and re-layouts  1.87 us

profile of v2, /device:TPU:49, one launch (start us, length us, event | category | flops | bytes accessed | tf_op | source)
XLA Modules:
  0.0 92.6 jit_solution(5890499565764765953)
XLA Ops:
  0.0 90.8 %bags.1 = f32[1024,128]{1,0:T(8,128)} custom-call(s32[2,256]{1,0:T(2,128)} %bitcast.13, s32[32,2,128]{2,1,0:T(2,128)} %bitcast.11, s32[2,40,512]{2,1,0:T(8,128)} %bitcast.10, s32[2,512]{1,0:T(2,128)} %bitcast.12, f32[8192,1,128]{2,1,0:T(1,128)} %bitcast.8), custom_call_target="tpu_custom_call" | custom-call | tf_op jit(solution)/shard_map/bags/pallas_call | solution.py:376
  90.8 1.9 %copy.7 = f32[512,2,128]{2,1,0:T(2,128)} copy(f32[512,2,128]{2,1,0:T(2,128)} %bitcast.9) | data formatting | bytes 1048576

commit v3 on v2

--- a/solution.py
+++ b/solution.py
@@ -12,13 +12,15 @@
 CORES = 2
 FIELDS = 4
 BITS = 8
+CAP_BITS = 4
+Z_BITS = 3
 
 FAR = (
-    ((4, -2, 1, 2), (5, -1, 1, 1), (3, 1, 2, 1), (6, 0, 1, 0), (2, 0, 2, 0)),
+    ((5, -1, 1, 1), (4, -2, 1, 2), (3, 1, 2, 1), (6, 0, 1, 0), (2, 0, 2, 0)),
     ((4, 2, 2, 2), (3, 1, 2, 1), (5, -1, 1, 1), (2, 0, 2, 0), (6, 0, 1, 0)),
 )
 NEAR = ((1, 1, 0, 0), (7, -1, 0, 2), (0, 0, 0, 1))
-ID_ORDER = (4, 5, 3, 6, 2, 1, 7, 0)
+ID_ORDER = (5, 4, 3, 6, 2, 1, 7, 0)
 
 
 def near_slot(b):
@@ -128,7 +130,7 @@
         to = (node_from[j], chip_at(-dy, -delta))
         pltpu.make_async_remote_copy(
             msg.at[to[0] * n_chip + to[1]],
-            idbuf.at[delta * q_all + dy * n_node + j],
+            idbuf[delta].at[dy * n_node + j],
             id_send,
             id_recv.at[delta],
             device_id=to,
@@ -151,6 +153,7 @@
         lax.fori_loop(0, ny, one, 0)
 
     position = lax.broadcasted_iota(jnp.int32, (depth, samples), 0)
+    code_copies = {}
     for t in range(tables):
         index = inv[t]
 
@@ -159,29 +162,27 @@
             return slot + jnp.where(index >= start[t, o] + n, cap - n, 0)
 
         slot = lax.fori_loop(0, owners - 1, shift, index, unroll=5)
-        plane = (slot // cap) % NZ
-        value = plane * slots + (slot // (cap * NZ)) * cap + slot % cap
-        code[t] = jnp.where(position < lens[pl.ds(t, 1), :], value, -1)
-    code_copies = []
-    for side, dz in ((0, 2), (1, -2)):
-        copy = pltpu.make_async_remote_copy(
-            code,
-            code_in[side],
-            code_send.at[side],
-            code_recv.at[side],
-            device_id=above(dz),
-            device_id_type=MESH,
-        )
-        copy.start()
-        code_copies.append(copy)
-
-    def split_codes(source, g):
-        for t in range(tables):
-            v = source[t]
-            live = v >= 0
-            inside = v % slots
-            group_of[g, t] = jnp.where(live, (v // slots) * words + inside % words, -1)
-            unit_of[g, t] = jnp.where(live, 1 << (BITS * (inside // words)), 0)
+        plane = (slot >> CAP_BITS) & (NZ - 1)
+        inside = (slot >> (CAP_BITS + Z_BITS)) * cap + (slot & (cap - 1))
+        code[t][...] = jnp.where(position < lens[pl.ds(t, 1), :], plane * slots + inside, -1)
+        for side, dz in ((0, 2), (1, -2)):
+            copy = pltpu.make_async_remote_copy(
+                code[t],
+                code_in[tables * side + t],
+                code_send.at[side, t],
+                code_recv.at[side, t],
+                device_id=above(dz),
+                device_id_type=MESH,
+            )
+            copy.start()
+            code_copies[side, t] = copy
+
+    def split_codes(source, g, t):
+        v = source[...]
+        live = v >= 0
+        inside = v & (slots - 1)
+        group_of[g, t] = jnp.where(live, (v // slots) * words + (inside & (words - 1)), -1)
+        unit_of[g, t] = jnp.where(live, 1 << (BITS * (inside // words)), 0)
 
     lanes = min(128, samples)
     rows_at = lax.broadcasted_iota(jnp.int32, (words, lanes), 0)
@@ -224,16 +225,17 @@
                 count(w, g, t, lax.rem(z + NZ + dz, NZ))
 
     def ids_ready(delta):
-        rows = pl.ds(delta * q_all, q_all) if delta else pl.ds(1, q_all - 1)
-        got = idbuf.at[rows]
+        rows = pl.ds(0, q_all) if delta else pl.ds(1, q_all - 1)
+        got = idbuf[delta].at[rows]
         pltpu.make_async_copy(got, got, id_recv.at[delta]).wait()
-        copy = pltpu.make_async_copy(got, idnum.at[rows], num_sem.at[delta])
+        copy = pltpu.make_async_copy(got, idnum[delta].at[rows], num_sem.at[delta])
         copy.start()
         return copy
 
-    def collect(k, t):
+    def collect(delta, i, t):
+        k = delta * q_all + i
         for s in range(cap):
-            r = idnum[k, 0, t * cap + s]
+            r = idnum[delta][i, 0, t * cap + s]
             send[k, t, pl.ds(s, 1), :] = table[t * rows_dev + r]
 
     def serve(delta, dz, slot, t):
@@ -255,7 +257,7 @@
                 k = delta * q_all + dy * n_node + j
                 for tt in range(tables):
                     if t is None or t == tt:
-                        collect(k, tt)
+                        collect(delta, dy * n_node + j, tt)
                 if dz == 0 and j == 0:
 
                     @pl.when(dy > 0)
@@ -274,18 +276,27 @@
         lax.fori_loop(0, ny, line, 0)
 
     def serve_far(t):
-        for delta, dz, g, b in FAR[t]:
+        for n, (delta, dz, g, b) in enumerate(FAR[t]):
+            if t == 0:
+                for ahead in ID_ORDER[n : n + 2] if n else ID_ORDER[:2]:
+                    if ahead not in asked:
+                        asked.add(ahead)
+                        copies[ahead] = ids_ready(ahead)
+                numbers_ready(delta)
             serve(delta, dz, far_slot(t, g, b), t)
 
     own_ids = pltpu.make_async_copy(
-        msg.at[pl.ds(node * n_chip + chip, 1)], idnum.at[pl.ds(0, 1)], num_sem.at[NZ]
+        msg.at[pl.ds(node * n_chip + chip, 1)], idnum[0].at[pl.ds(0, 1)], num_sem.at[NZ]
     )
     own_ids.start()
-    copies = [ids_ready(delta) for delta in ID_ORDER]
+    copies = {}
+    asked = set()
+
+    def numbers_ready(delta):
+        if delta in copies:
+            copies.pop(delta).wait()
+
     fetch.wait()
-    own_ids.wait()
-    for copy in copies:
-        copy.wait()
 
     def rows_ready(slot):
         got = recv[slot]
@@ -322,19 +333,23 @@
             copy.start()
             part_copies.append((t, copy))
 
-    serve_far(0)
-    for g in (1, 2):
-        code_copies[g - 1].wait_recv()
-        split_codes(code_in[g - 1], g)
-        count_all(g, 0)
-    serve_far(1)
-    for g in (1, 2):
-        count_all(g, 1)
+    for t in range(tables):
+        serve_far(t)
+        for g in ((1, 2), (2, 1))[t]:
+            code_copies[g - 1, t].wait_recv()
+            split_codes(code_in[tables * (g - 1) + t], g, t)
+            count_all(g, t)
     pool_far(0)
+    for delta in ID_ORDER[5:]:
+        if delta not in asked:
+            copies[delta] = ids_ready(delta)
+    own_ids.wait()
+    for delta in ID_ORDER[5:]:
+        numbers_ready(delta)
     for delta, dz, _, b in NEAR:
         serve(delta, dz, near_slot(b), None)
-    split_codes(code, 0)
     for t in range(tables):
+        split_codes(code[t], 0, t)
         count_all(0, t)
     pool_far(1)
 
@@ -351,7 +366,7 @@
             acc[t][...] + (part[t][...] + part[tables + t][...])
         ).T
 
-    for copy in code_copies:
+    for copy in code_copies.values():
         copy.wait_send()
     for _, copy in part_copies:
         copy.wait_send()
@@ -375,7 +390,7 @@
     far = pltpu.VMEM((q_all, cap, width), jnp.float32)
     out = pl.pallas_call(
         functools.partial(kernel, dims),
-        out_shape=jax.ShapeDtypeStruct((samples * tables, width), jnp.float32),
+        out_shape=pltpu.VMEM((samples * tables, width), jnp.float32),
         in_specs=[
             pl.BlockSpec(memory_space=pltpu.SMEM),
             vmem,
@@ -388,10 +403,10 @@
             pltpu.VMEM((tables * rows_dev, 1, width), jnp.float32),
             pltpu.SMEM((tables, owners), jnp.int32),
             pltpu.VMEM((owners, 1, 128), jnp.int32),
-            pltpu.VMEM((owners, 1, 128), jnp.int32),
-            pltpu.SMEM((owners, 1, 128), jnp.int32),
-            pltpu.VMEM((tables, depth, samples), jnp.int32),
-            [pltpu.VMEM((tables, depth, samples), jnp.int32)] * 2,
+            [pltpu.VMEM((q_all, 1, 128), jnp.int32)] * NZ,
+            [pltpu.SMEM((q_all, 1, 128), jnp.int32)] * NZ,
+            [pltpu.VMEM((depth, samples), jnp.int32)] * tables,
+            [pltpu.VMEM((depth, samples), jnp.int32)] * (2 * tables),
             pltpu.VMEM((3, tables, depth, samples), jnp.int32),
             pltpu.VMEM((3, tables, depth, samples), jnp.int32),
             pltpu.VMEM((16, slots, samples), jnp.bfloat16),
@@ -404,8 +419,8 @@
             pltpu.SemaphoreType.DMA,
             pltpu.SemaphoreType.DMA((NZ,)),
             pltpu.SemaphoreType.DMA((NZ + 1,)),
-            pltpu.SemaphoreType.DMA((2,)),
-            pltpu.SemaphoreType.DMA((2,)),
+            pltpu.SemaphoreType.DMA((2, 2)),
+            pltpu.SemaphoreType.DMA((2, 2)),
             pltpu.SemaphoreType.DMA,
             pltpu.SemaphoreType.DMA((13,)),
             pltpu.SemaphoreType.DMA((2, 2)),

time: 92.8 us -> 89.8 us (0.968)
  the two profiles are of different devices: /device:TPU:49 before, /device:TPU:1 now
where the time goes in v3:
time: 89.8 us; the launch traced here: 89.7 us
  Pallas kernels  88.9 us (99%)
    pallas_call x1, Pallas kernels, local(): pl.pallas_call(functools.partial(kernel, dims), out_shape=pltpu.VMEM((sam...  88.9 us

profile of v3, /device:TPU:1, one launch (start us, length us, event | category | flops | bytes accessed | tf_op | source)
XLA Modules:
  0.0 89.7 jit_solution(12540342050474593482)
XLA Ops:
  0.0 88.9 %bags.1 = f32[1024,128]{1,0:T(8,128)S(1)} custom-call(s32[2,256]{1,0:T(2,128)} %bitcast.13, s32[32,2,128]{2,1,0:T(2,128)} %bitcast.11, s32[2,40,512]{2,1,0:T(8,128)} %bitcast.10, s32[2,512]{1,0:T(2,128)} %bitcast.12, f32[8192,1,128]{2,1,0:T(1,128)} %bitcast.9), custom_call_target="tpu_custom_call" | custom-call | tf_op jit(solution)/shard_map/bags/pallas_call | solution.py:391
  88.9 0.8 copy.7

commit v4 on v3

--- a/solution.py
+++ b/solution.py
@@ -19,12 +19,15 @@
     ((5, -1, 1, 1), (4, -2, 1, 2), (3, 1, 2, 1), (6, 0, 1, 0), (2, 0, 2, 0)),
     ((4, 2, 2, 2), (3, 1, 2, 1), (5, -1, 1, 1), (2, 0, 2, 0), (6, 0, 1, 0)),
 )
-NEAR = ((1, 1, 0, 0), (7, -1, 0, 2), (0, 0, 0, 1))
+NEAR = (
+    (1, 3, 0, 0, 7, 0),
+    (2, 4, 0, 0, 1, 0),
+    (3, 0, 1, -1, 1, 1),
+    (4, 0, 1, 1, 7, -1),
+    (0, 0, 0, 0, 0, 0),
+    (5, 0, 1, 0, 0, 0),
+)
 ID_ORDER = (5, 4, 3, 6, 2, 1, 7, 0)
-
-
-def near_slot(b):
-    return b
 
 
 def far_slot(t, g, b):
@@ -54,6 +57,7 @@
     recv,
     acc,
     part,
+    inbox,
     ready,
     table_sem,
     id_send,
@@ -65,6 +69,8 @@
     row_recv,
     part_send,
     part_recv,
+    inbox_send,
+    inbox_recv,
 ):
     nx, ny, cap, rows_dev = dims
     q_all = nx * CORES * ny
@@ -165,10 +171,10 @@
         plane = (slot >> CAP_BITS) & (NZ - 1)
         inside = (slot >> (CAP_BITS + Z_BITS)) * cap + (slot & (cap - 1))
         code[t][...] = jnp.where(position < lens[pl.ds(t, 1), :], plane * slots + inside, -1)
-        for side, dz in ((0, 2), (1, -2)):
+        for side, dz in ((0, 2), (1, -2), (2, 1), (3, -1))[: 2 if t else 4]:
             copy = pltpu.make_async_remote_copy(
                 code[t],
-                code_in[tables * side + t],
+                code_in[2 * side + t if side < 2 else side + 2],
                 code_send.at[side, t],
                 code_recv.at[side, t],
                 device_id=above(dz),
@@ -212,9 +218,7 @@
 
         lax.fori_loop(0, samples // lanes, tile, 0)
 
-    works = []
-    for b in range(3):
-        works += [(near_slot(b), 0, t, 2 * b + t, b - 1) for t in range(tables)]
+    works = [(slot, g, t, n, dz) for n, (slot, g, t, dz, _, _) in enumerate(NEAR)]
     for t in range(tables):
         for _, _, g, b in FAR[t]:
             works.append((far_slot(t, g, b), g, t, len(works), b if g == 1 else -b))
@@ -240,7 +244,7 @@
 
     def serve(delta, dz, slot, t):
         def piece(k):
-            return send.at[k] if t is None else send.at[k, t]
+            return send.at[k, t]
 
         def send_rows(k, dy, j):
             pltpu.make_async_remote_copy(
@@ -255,9 +259,7 @@
         def line(dy, _):
             for j in range(n_node):
                 k = delta * q_all + dy * n_node + j
-                for tt in range(tables):
-                    if t is None or t == tt:
-                        collect(delta, dy * n_node + j, tt)
+                collect(delta, dy * n_node + j, t)
                 if dz == 0 and j == 0:
 
                     @pl.when(dy > 0)
@@ -302,8 +304,11 @@
         got = recv[slot]
         pltpu.make_async_copy(got, got, row_recv.at[slot]).wait()
 
+    def acc_at(g, t):
+        return 2 * g + t if g < 3 else g + 3
+
     def pool(slot, g, t, w, first):
-        rows = recv[slot][:, t] if g == 0 else recv[slot][...]
+        rows = recv[slot][...]
         rows = rows.reshape(slots, 128).T
         high = rows.astype(jnp.bfloat16)
         low = (rows - high.astype(jnp.float32)).astype(jnp.bfloat16)
@@ -311,10 +316,11 @@
             jnp.concatenate([high, low], axis=0), weight[w], preferred_element_type=jnp.float32
         )
         new = both[:128] + both[128:]
-        total = acc[tables * g + t]
+        total = acc[acc_at(g, t)]
         total[...] = new if first else total[...] + new
 
     part_copies = []
+    inbox_copies = []
 
     def pool_far(t):
         for g in ((1, 2), (2, 1))[t]:
@@ -322,22 +328,46 @@
             for n, (slot, _, _, w, _) in enumerate(mine_now):
                 rows_ready(slot)
                 pool(slot, g, t, w, n == 0)
-            copy = pltpu.make_async_remote_copy(
-                acc[tables * g + t],
-                part[tables * (g - 1) + t],
-                part_send.at[g - 1, t],
-                part_recv.at[g - 1, t],
-                device_id=above(-2 if g == 1 else 2),
-                device_id_type=MESH,
-            )
-            copy.start()
-            part_copies.append((t, copy))
+            if t == 0:
+                copy = pltpu.make_async_remote_copy(
+                    acc[2 * g],
+                    inbox[g - 1],
+                    inbox_send.at[g - 1],
+                    inbox_recv.at[g - 1],
+                    device_id=above(-1 if g == 1 else 1),
+                    device_id_type=MESH,
+                )
+                copy.start()
+                inbox_copies.append(copy)
+            else:
+                send_part(acc[2 * g + 1], g - 1, t, -2 if g == 1 else 2)
+
+    def send_part(total, side, t, dz):
+        copy = pltpu.make_async_remote_copy(
+            total,
+            part[2 * side + t],
+            part_send.at[side, t],
+            part_recv.at[side, t],
+            device_id=above(dz),
+            device_id_type=MESH,
+        )
+        copy.start()
+        part_copies.append((t, copy))
+
+    def pool_next(g):
+        slot, _, t, w, _ = [work for work in works if work[1] == g][0]
+        rows_ready(slot)
+        pool(slot, g, t, w, True)
+        inbox_copies[g - 3].wait_recv()
+        total = acc[acc_at(g, t)]
+        total[...] = total[...] + inbox[g - 3][...]
+        send_part(total, g - 3, 0, -1 if g == 3 else 1)
 
     for t in range(tables):
         serve_far(t)
         for g in ((1, 2), (2, 1))[t]:
             code_copies[g - 1, t].wait_recv()
-            split_codes(code_in[tables * (g - 1) + t], g, t)
+            split_codes(code_in[2 * (g - 1) + t], g, t)
             count_all(g, t)
     pool_far(0)
     for delta in ID_ORDER[5:]:
@@ -346,18 +376,25 @@
     own_ids.wait()
     for delta in ID_ORDER[5:]:
         numbers_ready(delta)
-    for delta, dz, _, b in NEAR:
-        serve(delta, dz, near_slot(b), None)
+    for slot, _, t, _, delta, dz in NEAR:
+        serve(delta, dz, slot, t)
+    for g in (3, 4):
+        code_copies[g - 1, 0].wait_recv()
+        split_codes(code_in[g + 1], g, 0)
+        count_all(g, 0)
     for t in range(tables):
         split_codes(code[t], 0, t)
         count_all(0, t)
     pool_far(1)
-
-    for n, b in enumerate((1, 0, 2)):
-        rows_ready(near_slot(b))
-        for slot, g, t, w, _ in works:
-            if g == 0 and slot == near_slot(b):
-                pool(slot, g, t, w, n == 0)
+    pool_next(3)
+    pool_next(4)
+
+    done = set()
+    for slot, g, t, w, _ in works[: len(NEAR)]:
+        if g == 0:
+            rows_ready(slot)
+            pool(slot, g, t, w, t not in done)
+            done.add(t)
     for t in range(tables):
         for tt, copy in part_copies:
             if tt == t:
@@ -370,8 +407,10 @@
         copy.wait_send()
     for _, copy in part_copies:
         copy.wait_send()
+    for copy in inbox_copies:
+        copy.wait_send()
     pltpu.make_async_copy(msg.at[pl.ds(1, owners - 1)], msg.at[pl.ds(1, owners - 1)], id_send).wait()
-    sent = send.at[pl.ds(0, owners - 3)]
+    sent = send.at[pl.ds(0, owners - 4)]
     pltpu.make_async_copy(sent, sent, row_send).wait()
 
 
@@ -386,7 +425,6 @@
     slots = q_all * cap
     dims = (nx, ny, cap, rows_dev)
     vmem = pl.BlockSpec(memory_space=pltpu.VMEM)
-    block = pltpu.VMEM((q_all, tables, cap, width), jnp.float32)
     far = pltpu.VMEM((q_all, cap, width), jnp.float32)
     out = pl.pallas_call(
         functools.partial(kernel, dims),
@@ -406,25 +444,28 @@
             [pltpu.VMEM((q_all, 1, 128), jnp.int32)] * NZ,
             [pltpu.SMEM((q_all, 1, 128), jnp.int32)] * NZ,
             [pltpu.VMEM((depth, samples), jnp.int32)] * tables,
-            [pltpu.VMEM((depth, samples), jnp.int32)] * (2 * tables),
-            pltpu.VMEM((3, tables, depth, samples), jnp.int32),
-            pltpu.VMEM((3, tables, depth, samples), jnp.int32),
+            [pltpu.VMEM((depth, samples), jnp.int32)] * 6,
+            pltpu.VMEM((5, tables, depth, samples), jnp.int32),
+            pltpu.VMEM((5, tables, depth, samples), jnp.int32),
             pltpu.VMEM((16, slots, samples), jnp.bfloat16),
             pltpu.VMEM((owners, tables, cap, width), jnp.float32),
-            [block] * 3 + [far] * 10,
-            [pltpu.VMEM((width, samples), jnp.float32)] * (3 * tables),
+            [far] * 16,
+            [pltpu.VMEM((width, samples), jnp.float32)] * 8,
             [pltpu.VMEM((width, samples), jnp.float32)] * (2 * tables),
+            [pltpu.VMEM((width, samples), jnp.float32)] * 2,
             pltpu.SemaphoreType.REGULAR,
             pltpu.SemaphoreType.DMA,
             pltpu.SemaphoreType.DMA,
             pltpu.SemaphoreType.DMA((NZ,)),
             pltpu.SemaphoreType.DMA((NZ + 1,)),
+            pltpu.SemaphoreType.DMA((4, 2)),
+            pltpu.SemaphoreType.DMA((4, 2)),
+            pltpu.SemaphoreType.DMA,
+            pltpu.SemaphoreType.DMA((16,)),
             pltpu.SemaphoreType.DMA((2, 2)),
             pltpu.SemaphoreType.DMA((2, 2)),
-            pltpu.SemaphoreType.DMA,
-            pltpu.SemaphoreType.DMA((13,)),
-            pltpu.SemaphoreType.DMA((2, 2)),
-            pltpu.SemaphoreType.DMA((2, 2)),
+            pltpu.SemaphoreType.DMA((2,)),
+            pltpu.SemaphoreType.DMA((2,)),
         ],
         compiler_params=pltpu.CompilerParams(
             collective_id=0, has_side_effects=True, vmem_limit_bytes=56 << 20

time: 89.8 us -> 85.4 us (0.951)
  Pallas kernels: 88.9 us -> 84.5 us
    pallas_call x1, Pallas kernels: 88.9 us -> 84.5 us  [local(): pl.pallas_call(functools.partial(kernel, dims), out_shape=pltpu.VMEM((sam...]
where the time goes in v4:
time: 85.4 us
  Pallas kernels  84.5 us (99%)
    pallas_call x1, Pallas kernels, local(): pl.pallas_call(functools.partial(kernel, dims), out_shape=pltpu.VMEM((sam...  84.5 us

profile of v4, /device:TPU:1, one launch (start us, length us, event | category | flops | bytes accessed | tf_op | source)
XLA Modules:
  0.0 85.4 jit_solution(5184041001703549867)
XLA Ops:
  0.0 84.5 %bags.1 = f32[1024,128]{1,0:T(8,128)S(1)} custom-call(s32[2,256]{1,0:T(2,128)} %bitcast.13, s32[32,2,128]{2,1,0:T(2,128)} %bitcast.11, s32[2,40,512]{2,1,0:T(8,128)} %bitcast.10, s32[2,512]{1,0:T(2,128)} %bitcast.12, f32[8192,1,128]{2,1,0:T(1,128)} %bitcast.9), custom_call_target="tpu_custom_call" | custom-call | tf_op jit(solution)/shard_map/bags/pallas_call | solution.py:429
  84.6 0.8 copy.7
